TPU v7x, 32 devices: a whole 2x2x4 slice. The times are simulated.
32 devices in a mesh: row: 8 (over z, y), col: 4 (over x, core).
Axes of the slice: x: 2, y: 2, z: 4, core: 2. Of those that a mesh axis runs over, the one named last changes fastest.
Arguments:
- eigvecs: float32 [32768, 512], P('row', 'col'), may hold values from -6 to 6
- reflectors: float32 [2, 32768, 512], P(None, 'row', 'col'), may hold values from -0.03125 to 0.03125
- factors: float32 [2, 512, 512], replicated, may hold values from -1 to 2, as said below
- slab: float32 [2048, 32768], P('col', 'row'), may hold values from -0.03125 to 0.03125
Outputs:
- vectors: float32 [32768, 512], P('row', 'col')
- product: float32 [2048, 512], P('col', 'row')
Inputs may be any that keep to these rules, and one draw needn't show every extreme that they name: Each of the two 512 x 512 factors is upper triangular, with diagonal entries between 1 and 2.
All inputs are finite; a program needn't handle non-finite values.
Results may differ from a plain program's by a relative error of at most 0.000088.
Values sent between devices are 32-bit elements; how exact they have to be, the bound alone decides.
A program may use at most 128 MiB of HBM per device.

v0:
```python
import functools

import jax
import jax.numpy as jnp
from jax import lax
from jax.experimental import pallas as pl
from jax.experimental.pallas import tpu as pltpu
from jax.sharding import PartitionSpec as P

MESH = pl.DeviceIdType.MESH
NN = ((1,), (0,))
NT = ((1,), (1,))
TN = ((0,), (0,))


def dot(left, right, dims=NN):
    return lax.dot_general(
        left, right, (dims, ((), ())), precision=lax.Precision.HIGH, preferred_element_type=jnp.float32
    )


def tdot(left, right):
    return dot(left, right, TN)


def halves(a):
    high = a.astype(jnp.bfloat16)
    return high, (a - high.astype(jnp.float32)).astype(jnp.bfloat16)


def dot3(left, right, dims):
    def one(a, b):
        return lax.dot_general(a, b, (dims, ((), ())), preferred_element_type=jnp.float32)

    (lh, ll), (rh, rl) = left, right
    return one(lh, rh) + (one(lh, rl) + one(ll, rh))


def loop(lo, hi, body):
    if hi - lo == 1:
        body(lo)
    elif hi > lo:
        lax.fori_loop(lo, hi, lambda i, carry: (body(i), carry)[1], 0)


def aligned(i, size):
    return pl.ds(pl.multiple_of(i * size, size), size)


def whole_kernel(
    dims, x_hbm, y_hbm, t_hbm, s_hbm, vec_hbm, out_ref,
    xb, y1b, y2b, sb, tb, vb, w, wf, tw, ybuf, zbuf, xs, xr, pacc, pt, pyb, pzb,
    lx, ly, ls, px_s, px_r, py_s, py_r, m_s, m_r, f_s, f_r,
    ry_s, ry_r, rz_s, rz_r, rx_s, rx_r, gz_s, gz_r, gy_s, gy_r,
    vp_s, vp_r, vm_s, vm_r, vo,
):
    nz, q, nq, early, late = dims
    extra = early + late
    held = nq + extra
    bw = x_hbm.shape[1]
    r, c = lax.axis_index("row"), lax.axis_index("col")
    z, y = r // 2, lax.rem(r, 2)
    x, k = c // 2, lax.rem(c, 2)
    mate = (r, c + 1 - 2 * k)
    peer = (r, c + 2 - 4 * x)
    peer_block = c + 2 - 4 * x
    ynext = (r + 1 - 2 * y, c)

    def zat(d):
        return lax.rem(z + d, nz)

    def znext(d):
        return (zat(d) * 2 + y, c)

    partners = [mate, peer, ynext] + [znext(d) for d in range(1, nz)]
    barrier = pltpu.get_barrier_semaphore()
    for other in partners:
        pl.semaphore_signal(barrier, inc=1, device_id=other, device_id_type=MESH)
    pl.semaphore_wait(barrier, len(partners))

    def send(src, dst, s, t, device):
        return pltpu.make_async_remote_copy(src, dst, s, t, device_id=device, device_id_type=MESH)

    def chunk(i):
        return aligned(i, q)

    def place(i, side):
        within = lax.rem(i, nq)
        half = jnp.where(i < nq, side, 1 - side)
        return pl.ds(pl.multiple_of((half * nq + within) * q, q), q)

    def lanes(b):
        return aligned(b, bw)

    panels = (y1b, y2b)

    def x_local(i):
        return pltpu.make_async_copy(x_hbm.at[place(i, x)], xb.at[chunk(i), lanes(x)], lx.at[i])

    def x_peer(i):
        return send(x_hbm.at[place(i, 1 - x)], xb.at[chunk(i), lanes(x)], px_s.at[i], px_r.at[i], peer)

    def y_local(p, i):
        return pltpu.make_async_copy(y_hbm.at[p, place(i, x)], panels[p].at[chunk(i), lanes(c)], ly.at[p, i])

    def y_peer(p, i):
        return send(
            y_hbm.at[p, place(i, 1 - x)], panels[p].at[chunk(i), lanes(c)], py_s.at[p, i], py_r.at[p, i], peer)

    def y_mate(p, i):
        return send(y_hbm.at[p, place(i, x)], panels[p].at[chunk(i), lanes(c)], m_s.at[p, i], m_r.at[p, i], mate)

    def y_forward(p, i):
        block = panels[p].at[chunk(i), lanes(peer_block)]
        return send(block, block, f_s.at[p, i], f_r.at[p, i], mate)

    def wait_x(i):
        x_local(i).wait()
        x_peer(i).wait_recv()

    def wait_y(p, i):
        y_local(p, i).wait()
        y_mate(p, i).wait_recv()
        y_forward(p, i).wait_recv()

    def pass_on(p, i):
        y_peer(p, i).wait_recv()
        y_forward(p, i).start()

    def send_bulk(i):
        x_peer(i).start()
        y_peer(1, i).start()
        y_peer(0, i).start()

    def first_two(i):
        x_peer(i).start()
        y_peer(1, i).start()

    loop(0, nq, first_two)
    loop(0, nq, lambda i: y_peer(0, i).start())

    def own(i):
        x_local(i).start()
        y_mate(1, i).start()
        y_local(1, i).start()
        y_mate(0, i).start()
        y_local(0, i).start()

    loop(0, held, own)
    t_copy = pltpu.make_async_copy(t_hbm, tb, ls.at[0])
    s_copy = pltpu.make_async_copy(s_hbm, sb, ls.at[1])
    t_copy.start()
    s_copy.start()

    w[...] = jnp.zeros_like(w)
    pacc[...] = jnp.zeros_like(pacc)

    def step(i):
        @pl.when(i < nq)
        def _():
            pass_on(1, i)

        @pl.when(i > 0)
        def _():
            j = i - 1
            wait_x(j)
            wait_y(1, j)
            w[0] += dot3(halves(xb[chunk(j), :]), halves(y2b[chunk(j), :]), TN)

    loop(0, nq + 1, step)
    t_copy.wait()
    s_copy.wait()

    rows = w.shape[1] // (2 * nz)

    def sum_rows(n, piece, ys, zs):
        order = list(range(1, nz)) + [0]
        out = [send(piece(zat(d), 1 - y), ys.at[d], ry_s.at[n, d], ry_r.at[n, d], ynext) for d in order]
        for copy in out:
            copy.start()
        hops = []
        for d, copy in zip(order, out):
            copy.wait_recv()
            mine = piece(zat(d), y)
            if d:
                mine[...] += ys[d]
                hops.append(send(mine, zs.at[d], rz_s.at[n, d], rz_r.at[n, d], znext(d)))
                hops[-1].start()
            else:
                total = mine[...] + ys[0]
        for d, copy in zip(order, hops):
            copy.wait_recv()
            total = total + zs[d]
        return total, out + hops

    def all_sum(n, after_exchange, before_last):
        def piece(zz, yy):
            return w.at[n, aligned(zz * 2 + yy, rows)]

        def final(zz, yy):
            return wf.at[n, aligned(zz * 2 + yy, rows)]

        total, sent = sum_rows(n, piece, ybuf.at[n], zbuf.at[n])
        xs[n] = total
        swap = send(xs.at[n], xr.at[n], rx_s.at[n], rx_r.at[n], peer)
        swap.start()
        after_exchange()
        swap.wait_recv()
        mine = final(z, y)
        mine[...] = xs[n] + xr[n]
        along = [send(mine, mine, gz_s.at[n, d], gz_r.at[n, d], znext(d)) for d in range(1, nz)]
        for copy in along:
            copy.start()
        across = [send(mine, mine, gy_s.at[n, 0], gy_r.at[n, 0], ynext)]
        across[0].start()
        for d in range(1, nz):
            along[d - 1].wait_recv()
            block = final(lax.rem(z + nz - d, nz), y)
            across.append(send(block, block, gy_s.at[n, d], gy_r.at[n, d], ynext))
            across[-1].start()
        before_last()
        for copy in across:
            copy.wait_recv()
        return sent + [swap] + along + across

    def inner(i):
        xb[chunk(i), :] = xb[chunk(i), :] - dot3(halves(y2b[chunk(i), :]), halves(tw[1]), NN)

    def apply(p, n):
        tw[p] = dot3(halves(tb[p]), halves(wf[n]), NT)

    sent = all_sum(0, lambda: loop(nq, nq + early, send_bulk), lambda: loop(0, nq, lambda i: pass_on(0, i)))
    apply(1, 0)

    def second(i):
        inner(i)
        wait_y(0, i)
        w[1] += dot3(halves(xb[chunk(i), :]), halves(y1b[chunk(i), :]), TN)

    loop(0, nq, second)

    def take_extra(i):
        pass_on(1, i)
        pass_on(0, i)

    def extra_inner(i):
        wait_x(i)
        wait_y(1, i)
        inner(i)

    def early_extra():
        loop(nq, nq + early, take_extra)
        loop(nq, nq + early, extra_inner)

    sent += all_sum(1, lambda: loop(nq + early, held, send_bulk), early_extra)
    apply(0, 1)

    def v_mate(i):
        block = vb.at[k, chunk(i)]
        return send(block, block, vm_s.at[i], vm_r.at[i], mate)

    def v_peer(i):
        return send(vb.at[k, chunk(i)], vb.at[k, chunk(i + nq)], vp_s.at[i], vp_r.at[i], peer)

    def v_out(i):
        return pltpu.make_async_copy(vb.at[k, chunk(i), lanes(x)], vec_hbm.at[place(i, x)], vo.at[i])

    def finish(i):
        vb[k, chunk(i), :] = xb[chunk(i), :] - dot3(halves(y1b[chunk(i), :]), halves(tw[0]), NN)

    def ship(i):
        v_mate(i).start()
        v_out(i).start()

    def finish_sent(i):
        finish(i)
        v_peer(i).start()
        ship(i)

    def finish_kept(i):
        finish(i)
        ship(i)

    def finish_extra(i):
        wait_y(0, i)
        finish(i)
        ship(i)

    loop(extra, nq, finish_sent)
    loop(nq + early, held, take_extra)
    loop(0, extra, finish_kept)
    loop(nq + early, held, extra_inner)
    loop(nq, held, finish_extra)

    def columns(i):
        return halves(sb[:, place(i, x)])

    def multiply(i):
        v_mate(i).wait_recv()
        part = columns(i)
        for h in range(2):
            pacc[h] += dot3(part, halves(vb[h, chunk(i), :]), NN)

    def multiply_far(i):
        v_peer(i - nq).wait_recv()
        ship(i)
        part = columns(i)
        pacc[k] += dot3(part, halves(vb[k, chunk(i), :]), NN)
        v_mate(i).wait_recv()
        pacc[1 - k] += dot3(part, halves(vb[1 - k, chunk(i), :]), NN)

    loop(0, held, multiply)
    loop(held, 2 * nq, multiply_far)

    for h in range(2):
        for side in range(2):
            pt[h + 2 * side] = pacc[h, :, side * bw : (side + 1) * bw].T

    share = out_ref.shape[0]
    total, last = sum_rows(2, lambda zz, yy: pt.at[zz, aligned(yy, share)], pyb, pzb)
    out_ref[...] = total

    for copy in sent + last:
        copy.wait_send()

    def drain(i):
        x_peer(i).wait_send()
        for p in range(2):
            y_peer(p, i).wait_send()
            y_mate(p, i).wait_send()
            y_forward(p, i).wait_send()

    loop(0, held, drain)
    loop(extra, nq, lambda i: v_peer(i).wait_send())

    def drain_v(i):
        v_mate(i).wait_send()
        v_out(i).wait()

    loop(0, 2 * nq, drain_v)


CHUNK = 512
EARLY, LATE = 1, 1


def on_grid(nrow, ncol, eigvecs, reflectors, factors, slab):
    size, bw = eigvecs.shape
    panel = factors.shape[1]
    nz = nrow // 2
    half = size // 2
    q = min(CHUNK, half)
    nq = half // q
    early, late = min(EARLY, nq), min(LATE, nq - min(EARLY, nq))
    extra = early + late
    held = nq + extra
    kept = held * q
    wide = 2 * bw
    f32 = jnp.float32
    rows = wide // nrow
    mine = slab.shape[0]
    share = ncol * bw // nrow
    sem = pltpu.SemaphoreType.DMA
    vmem = pltpu.VMEM
    vectors, product = pl.pallas_call(
        functools.partial(whole_kernel, (nz, q, nq, early, late)),
        out_shape=(
            jax.ShapeDtypeStruct((size, bw), f32),
            jax.ShapeDtypeStruct((share, mine), f32),
        ),
        in_specs=[pl.BlockSpec(memory_space=pl.ANY)] * 4,
        out_specs=(pl.BlockSpec(memory_space=pl.ANY), pl.BlockSpec(memory_space=pltpu.VMEM)),
        scratch_shapes=[
            vmem((kept, wide), f32), vmem((kept, panel), f32), vmem((kept, panel), f32),
            vmem(slab.shape, f32), vmem(factors.shape, f32), vmem((2, size, wide), f32),
            vmem((2, wide, panel), f32), vmem((2, wide, panel), f32), vmem((2, panel, wide), f32),
            vmem((2, nz, rows, panel), f32), vmem((2, nz, rows, panel), f32),
            vmem((2, rows, panel), f32), vmem((2, rows, panel), f32),
            vmem((2, mine, wide), f32), vmem((nz, bw, mine), f32),
            vmem((nz, share, mine), f32), vmem((nz, share, mine), f32),
            sem((held,)), sem((2, held)), sem((2,)),
            sem((held,)), sem((held,)), sem((2, held)), sem((2, held)),
            sem((2, held)), sem((2, held)), sem((2, held)), sem((2, held)),
            sem((3, nz)), sem((3, nz)), sem((3, nz)), sem((3, nz)),
            sem((2,)), sem((2,)),
            sem((2, nz)), sem((2, nz)), sem((2, nz)), sem((2, nz)),
            sem((nq,)), sem((nq,)), sem((2 * nq,)), sem((2 * nq,)), sem((2 * nq,)),
        ],
        compiler_params=pltpu.CompilerParams(
            collective_id=0, has_side_effects=True, vmem_limit_bytes=66_000_000),
        name="whole",
    )(eigvecs, reflectors, factors, slab)
    return vectors, product.T


def on_any(nrow, ncol, eigvecs, reflectors, factors, slab):
    c = lax.axis_index("col")
    first_own, second_own = reflectors[0], reflectors[1]
    all_x, second_y, first_y = (
        lax.all_gather(block, "col", axis=1, tiled=True) for block in (eigvecs, second_own, first_own)
    )
    own = second_own.shape[1]
    both = jnp.concatenate([second_own, first_own], axis=1)
    stacked = jnp.concatenate([tdot(both, all_x), tdot(first_own, second_y)])
    slab_x, slab_second, slab_first = (dot(block, slab, ((0,), (1,))) for block in (all_x, second_y, first_y))
    sums = lax.all_gather(lax.psum(stacked, "row"), "col")
    panel = factors.shape[1]
    second_w, first_raw, gram = (sums[:, i * own : (i + 1) * own].reshape(panel, -1) for i in range(3))
    second_tw = dot(factors[1], second_w)
    first_tw = dot(factors[0], first_raw - dot(gram, second_tw))
    partial = slab_x - tdot(second_tw, slab_second) - tdot(first_tw, slab_first)
    product = lax.psum_scatter(partial, "row", tiled=True)
    vectors = eigvecs
    for block, tw in ((second_y, second_tw), (first_y, first_tw)):
        width = eigvecs.shape[1]
        vectors = vectors - dot(block, lax.dynamic_slice_in_dim(tw, c * width, width, axis=1))
    return vectors, product.T


def solution(mesh):
    nrow, ncol = mesh.shape["row"], mesh.shape["col"]
    fits = ncol == 4 and nrow == 2 * ncol
    return jax.shard_map(
        functools.partial(on_grid if fits else on_any, nrow, ncol),
        mesh=mesh,
        in_specs=(P("row", "col"), P(None, "row", "col"), P(), P("col", "row")),
        out_specs=(P("row", "col"), P("col", "row")),
        check_vma=False,
    )
```

profile of v0, /device:TPU:0, one launch (start us, length us, event | category | flops | bytes accessed | tf_op | source)
XLA Modules:
  0.0 171.0 jit_solution(13992596971516776184)
XLA Ops:
  0.6 166.6 %whole.1 = (f32[4096,128]{1,0:T(8,128)}, f32[64,512]{1,0:T(8,128)}) custom-call(f32[4096,128]{1,0:T(8,128)} %x_hbm.1, f32[2,4096,128]{2,1,0:T(8,128)} %y_hbm.1, f32[2,512,512]{2,1,0:T(8,128)} %t_hbm.1, f32[512,4096]{1,0:T(8,128)} %s_hbm.1), custom_call_target="tpu_custom_call" | custom-call | tf_op jit(solution)/shard_map/whole/pallas_call | solution.py:365
  167.3 0.0 copy-start
  167.3 3.1 %copy.8 = f32[4096,128]{1,0:T(8,128)} copy(f32[4096,128]{1,0:T(8,128)} %get-tuple-element.8) | data formatting | bytes 4194304
  170.4 0.0 copy-done
  170.4 0.7 copy.9
Async XLA Ops:
  167.3 3.1 %copy-start = (f32[64,512]{1,0:T(8,128)S(1)}, f32[64,512]{1,0:T(8,128)}, u32[]{:S(2)}) copy-start(f32[64,512]{1,0:T(8,128)} %get-tuple-element.5) | copy-start | bytes 393220
where the time goes:
time: 172 us; the launch traced here: 171 us
  Pallas kernels  167 us (97%)
  local copies, waits for them, and re-layouts  3.74 us (2%)
    pallas_call x1, Pallas kernels, on_grid(): pl.pallas_call(functools.partial(whole_kernel, (nz, q, nq, early, late)),...  167 us
    unnamed x4, local copies, waits for them, and re-layouts  3.74 us

commit v1 on v0

--- a/solution.py
+++ b/solution.py
@@ -49,12 +49,12 @@
 
 def whole_kernel(
     dims, x_hbm, y_hbm, t_hbm, s_hbm, vec_hbm, out_ref,
-    xb, y1b, y2b, sb, tb, vb, w, wf, tw, ybuf, zbuf, xs, xr, pacc, pt, pyb, pzb,
+    xb, y1b, y2b, sb, tb, vb, w, gram, wf, tw, ybuf, zbuf, xs, xr, pacc, pt, pyb, pzb,
     lx, ly, ls, px_s, px_r, py_s, py_r, m_s, m_r, f_s, f_r,
     ry_s, ry_r, rz_s, rz_r, rx_s, rx_r, gz_s, gz_r, gy_s, gy_r,
     vp_s, vp_r, vm_s, vm_r, vo,
 ):
-    nz, q, nq, early, late = dims
+    nz, q, nq, ahead, early, late = dims
     extra = early + late
     held = nq + extra
     bw = x_hbm.shape[1]
@@ -137,7 +137,7 @@
         y_peer(1, i).start()
 
     loop(0, nq, first_two)
-    loop(0, nq, lambda i: y_peer(0, i).start())
+    loop(0, ahead, lambda i: y_peer(0, i).start())
 
     def own(i):
         x_local(i).start()
@@ -153,6 +153,7 @@
     s_copy.start()
 
     w[...] = jnp.zeros_like(w)
+    gram[...] = jnp.zeros_like(gram)
     pacc[...] = jnp.zeros_like(pacc)
 
     def step(i):
@@ -173,7 +174,7 @@
 
     rows = w.shape[1] // (2 * nz)
 
-    def sum_rows(n, piece, ys, zs):
+    def sum_rows(n, piece, ys, zs, meanwhile):
         order = list(range(1, nz)) + [0]
         out = [send(piece(zat(d), 1 - y), ys.at[d], ry_s.at[n, d], ry_r.at[n, d], ynext) for d in order]
         for copy in out:
@@ -188,19 +189,20 @@
                 hops[-1].start()
             else:
                 total = mine[...] + ys[0]
+        meanwhile()
         for d, copy in zip(order, hops):
             copy.wait_recv()
             total = total + zs[d]
         return total, out + hops
 
-    def all_sum(n, after_exchange, before_last):
+    def all_sum(n, meanwhile, after_exchange, after_sends, before_last):
         def piece(zz, yy):
             return w.at[n, aligned(zz * 2 + yy, rows)]
 
         def final(zz, yy):
             return wf.at[n, aligned(zz * 2 + yy, rows)]
 
-        total, sent = sum_rows(n, piece, ybuf.at[n], zbuf.at[n])
+        total, sent = sum_rows(n, piece, ybuf.at[n], zbuf.at[n], meanwhile)
         xs[n] = total
         swap = send(xs.at[n], xr.at[n], rx_s.at[n], rx_r.at[n], peer)
         swap.start()
@@ -213,6 +215,7 @@
             copy.start()
         across = [send(mine, mine, gy_s.at[n, 0], gy_r.at[n, 0], ynext)]
         across[0].start()
+        after_sends()
         for d in range(1, nz):
             along[d - 1].wait_recv()
             block = final(lax.rem(z + nz - d, nz), y)
@@ -229,15 +232,26 @@
     def apply(p, n):
         tw[p] = dot3(halves(tb[p]), halves(wf[n]), NT)
 
-    sent = all_sum(0, lambda: loop(nq, nq + early, send_bulk), lambda: loop(0, nq, lambda i: pass_on(0, i)))
+    def raw(i):
+        wait_y(0, i)
+        first = halves(y1b[chunk(i), :])
+        w[1] += dot3(halves(xb[chunk(i), :]), first, TN)
+        gram[...] += dot3(halves(y2b[chunk(i), :]), first, TN)
+
+    def rest():
+        loop(ahead, nq, lambda i: y_peer(0, i).start())
+        loop(nq, nq + early, send_bulk)
+        loop(0, nq - 2, lambda i: pass_on(0, i))
+        loop(0, nq - 2, raw)
+
+    def nearly():
+        pass_on(0, nq - 2)
+        raw(nq - 2)
+
+    sent = all_sum(0, lambda: None, rest, nearly, lambda: pass_on(0, nq - 1))
     apply(1, 0)
-
-    def second(i):
-        inner(i)
-        wait_y(0, i)
-        w[1] += dot3(halves(xb[chunk(i), :]), halves(y1b[chunk(i), :]), TN)
-
-    loop(0, nq, second)
+    raw(nq - 1)
+    w[1] = w[1] - dot3(halves(tw[1]), halves(gram[...]), TN)
 
     def take_extra(i):
         pass_on(1, i)
@@ -252,7 +266,8 @@
         loop(nq, nq + early, take_extra)
         loop(nq, nq + early, extra_inner)
 
-    sent += all_sum(1, lambda: loop(nq + early, held, send_bulk), early_extra)
+    sent += all_sum(
+        1, lambda: loop(0, nq, inner), lambda: loop(nq + early, held, send_bulk), lambda: None, early_extra)
     apply(0, 1)
 
     def v_mate(i):
@@ -317,11 +332,6 @@
             pt[h + 2 * side] = pacc[h, :, side * bw : (side + 1) * bw].T
 
     share = out_ref.shape[0]
-    total, last = sum_rows(2, lambda zz, yy: pt.at[zz, aligned(yy, share)], pyb, pzb)
-    out_ref[...] = total
-
-    for copy in sent + last:
-        copy.wait_send()
 
     def drain(i):
         x_peer(i).wait_send()
@@ -330,17 +340,25 @@
             y_mate(p, i).wait_send()
             y_forward(p, i).wait_send()
 
-    loop(0, held, drain)
-    loop(extra, nq, lambda i: v_peer(i).wait_send())
-
     def drain_v(i):
         v_mate(i).wait_send()
         v_out(i).wait()
 
-    loop(0, 2 * nq, drain_v)
+    def drain_all():
+        for copy in sent:
+            copy.wait_send()
+        loop(0, held, drain)
+        loop(extra, nq, lambda i: v_peer(i).wait_send())
+        loop(0, 2 * nq, drain_v)
+
+    total, last = sum_rows(2, lambda zz, yy: pt.at[zz, aligned(yy, share)], pyb, pzb, drain_all)
+    out_ref[...] = total
+    for copy in last:
+        copy.wait_send()
 
 
 CHUNK = 512
+AHEAD = 3
 EARLY, LATE = 1, 1
 
 
@@ -363,7 +381,7 @@
     sem = pltpu.SemaphoreType.DMA
     vmem = pltpu.VMEM
     vectors, product = pl.pallas_call(
-        functools.partial(whole_kernel, (nz, q, nq, early, late)),
+        functools.partial(whole_kernel, (nz, q, nq, min(AHEAD, nq), early, late)),
         out_shape=(
             jax.ShapeDtypeStruct((size, bw), f32),
             jax.ShapeDtypeStruct((share, mine), f32),
@@ -373,7 +391,7 @@
         scratch_shapes=[
             vmem((kept, wide), f32), vmem((kept, panel), f32), vmem((kept, panel), f32),
             vmem(slab.shape, f32), vmem(factors.shape, f32), vmem((2, size, wide), f32),
-            vmem((2, wide, panel), f32), vmem((2, wide, panel), f32), vmem((2, panel, wide), f32),
+            vmem((2, wide, panel), f32), vmem((panel, panel), f32), vmem((2, wide, panel), f32), vmem((2, panel, wide), f32),
             vmem((2, nz, rows, panel), f32), vmem((2, nz, rows, panel), f32),
             vmem((2, rows, panel), f32), vmem((2, rows, panel), f32),
             vmem((2, mine, wide), f32), vmem((nz, bw, mine), f32),

time: 172 us -> 163 us (0.948)
  Pallas kernels: 167 us -> 157 us
    pallas_call x1, Pallas kernels: 167 us -> 157 us  [on_grid(): pl.pallas_call(functools.partial(whole_kernel, (nz, q, nq, min(AHEAD, nq)...]
where the time goes in v1:
time: 163 us; the launch traced here: 162 us
  Pallas kernels  157 us (96%)
  local copies, waits for them, and re-layouts  3.74 us (2%)
    pallas_call x1, Pallas kernels, on_grid(): pl.pallas_call(functools.partial(whole_kernel, (nz, q, nq, min(AHEAD, nq)...  157 us
    unnamed x4, local copies, waits for them, and re-layouts  3.74 us

profile of v1, /device:TPU:0, one launch (start us, length us, event | category | flops | bytes accessed | tf_op | source)
XLA Modules:
  0.0 161.7 jit_solution(16145755915629855952)
XLA Ops:
  0.6 157.3 %whole.1 = (f32[4096,128]{1,0:T(8,128)}, f32[64,512]{1,0:T(8,128)}) custom-call(f32[4096,128]{1,0:T(8,128)} %x_hbm.1, f32[2,4096,128]{2,1,0:T(8,128)} %y_hbm.1, f32[2,512,512]{2,1,0:T(8,128)} %t_hbm.1, f32[512,4096]{1,0:T(8,128)} %s_hbm.1), custom_call_target="tpu_custom_call" | custom-call | tf_op jit(solution)/shard_map/whole/pallas_call | solution.py:383
  158.0 0.0 copy-start
  158.0 3.1 %copy.8 = f32[4096,128]{1,0:T(8,128)} copy(f32[4096,128]{1,0:T(8,128)} %get-tuple-element.8) | data formatting | bytes 4194304
  161.1 0.0 copy-done
  161.1 0.7 copy.9
Async XLA Ops:
  158.0 3.1 %copy-start = (f32[64,512]{1,0:T(8,128)S(1)}, f32[64,512]{1,0:T(8,128)}, u32[]{:S(2)}) copy-start(f32[64,512]{1,0:T(8,128)} %get-tuple-element.5) | copy-start | bytes 393220

commit v2 on v1

--- a/solution.py
+++ b/solution.py
@@ -49,15 +49,19 @@
 
 def whole_kernel(
     dims, x_hbm, y_hbm, t_hbm, s_hbm, vec_hbm, out_ref,
-    xb, y1b, y2b, sb, tb, vb, w, gram, wf, tw, ybuf, zbuf, xs, xr, pacc, pt, pyb, pzb,
+    xb, xt, y1b, y2b, sb, tb, vt, vst, w, gram, wf, tw, ybuf, zbuf, xs, xr, pt, pyb, pzb,
     lx, ly, ls, px_s, px_r, py_s, py_r, m_s, m_r, f_s, f_r,
     ry_s, ry_r, rz_s, rz_r, rx_s, rx_r, gz_s, gz_r, gy_s, gy_r,
     vp_s, vp_r, vm_s, vm_r, vo,
 ):
     nz, q, nq, ahead, early, late = dims
+    groups = pt.shape[0]
     extra = early + late
     held = nq + extra
     bw = x_hbm.shape[1]
+    share = out_ref.shape[0]
+    part = share // groups
+    span = xt.shape[0] // groups
     r, c = lax.axis_index("row"), lax.axis_index("col")
     z, y = r // 2, lax.rem(r, 2)
     x, k = c // 2, lax.rem(c, 2)
@@ -114,10 +118,6 @@
         block = panels[p].at[chunk(i), lanes(peer_block)]
         return send(block, block, f_s.at[p, i], f_r.at[p, i], mate)
 
-    def wait_x(i):
-        x_local(i).wait()
-        x_peer(i).wait_recv()
-
     def wait_y(p, i):
         y_local(p, i).wait()
         y_mate(p, i).wait_recv()
@@ -154,7 +154,20 @@
 
     w[...] = jnp.zeros_like(w)
     gram[...] = jnp.zeros_like(gram)
-    pacc[...] = jnp.zeros_like(pacc)
+    pt[...] = jnp.zeros_like(pt)
+
+    def pieces(block, side):
+        for g in range(groups):
+            for half in range(bw // share):
+                yield block + half * share + g * part, g * span + (side * (bw // share) + half) * part
+
+    def turn(i):
+        x_local(i).wait()
+        x_peer(i).wait_recv()
+        turned = xb[chunk(i), :].T
+        for side in range(2):
+            for src, dst in pieces(side * bw, side):
+                xt[dst : dst + part, chunk(i)] = turned[src : src + part]
 
     def step(i):
         @pl.when(i < nq)
@@ -164,9 +177,9 @@
         @pl.when(i > 0)
         def _():
             j = i - 1
-            wait_x(j)
+            turn(j)
             wait_y(1, j)
-            w[0] += dot3(halves(xb[chunk(j), :]), halves(y2b[chunk(j), :]), TN)
+            w[0] += dot3(halves(xt[:, chunk(j)]), halves(y2b[chunk(j), :]), NN)
 
     loop(0, nq + 1, step)
     t_copy.wait()
@@ -174,26 +187,33 @@
 
     rows = w.shape[1] // (2 * nz)
 
-    def sum_rows(n, piece, ys, zs, meanwhile):
-        order = list(range(1, nz)) + [0]
-        out = [send(piece(zat(d), 1 - y), ys.at[d], ry_s.at[n, d], ry_r.at[n, d], ynext) for d in order]
-        for copy in out:
-            copy.start()
-        hops = []
-        for d, copy in zip(order, out):
-            copy.wait_recv()
-            mine = piece(zat(d), y)
-            if d:
-                mine[...] += ys[d]
-                hops.append(send(mine, zs.at[d], rz_s.at[n, d], rz_r.at[n, d], znext(d)))
-                hops[-1].start()
-            else:
-                total = mine[...] + ys[0]
-        meanwhile()
-        for d, copy in zip(order, hops):
-            copy.wait_recv()
-            total = total + zs[d]
-        return total, out + hops
+    class Sum:
+        def __init__(self, n, piece, ys, zs):
+            self.order = list(range(1, nz)) + [0]
+            self.piece, self.zs, self.ys = piece, zs, ys
+            self.out = [
+                send(piece(zat(d), 1 - y), ys.at[d], ry_s.at[n, d], ry_r.at[n, d], ynext) for d in self.order]
+            self.hops = [send(piece(zat(d), y), zs.at[d], rz_s.at[n, d], rz_r.at[n, d], znext(d)) for d in range(1, nz)]
+            for copy in self.out:
+                copy.start()
+
+        def relay(self):
+            for d, copy in zip(self.order, self.out):
+                copy.wait_recv()
+                if d:
+                    self.piece(zat(d), y)[...] += self.ys[d]
+                    self.hops[d - 1].start()
+
+        def total(self):
+            total = self.piece(z, y)[...] + self.ys[0]
+            for d in range(1, nz):
+                self.hops[d - 1].wait_recv()
+                total = total + self.zs[d]
+            return total
+
+        def wait_sends(self):
+            for copy in self.out + self.hops:
+                copy.wait_send()
 
     def all_sum(n, meanwhile, after_exchange, after_sends, before_last):
         def piece(zz, yy):
@@ -202,8 +222,10 @@
         def final(zz, yy):
             return wf.at[n, aligned(zz * 2 + yy, rows)]
 
-        total, sent = sum_rows(n, piece, ybuf.at[n], zbuf.at[n], meanwhile)
-        xs[n] = total
+        reduced = Sum(n, piece, ybuf.at[n], zbuf.at[n])
+        reduced.relay()
+        meanwhile()
+        xs[n] = reduced.total()
         swap = send(xs.at[n], xr.at[n], rx_s.at[n], rx_r.at[n], peer)
         swap.start()
         after_exchange()
@@ -224,18 +246,18 @@
         before_last()
         for copy in across:
             copy.wait_recv()
-        return sent + [swap] + along + across
+        return reduced.out + reduced.hops + [swap] + along + across
 
     def inner(i):
-        xb[chunk(i), :] = xb[chunk(i), :] - dot3(halves(y2b[chunk(i), :]), halves(tw[1]), NN)
+        xt[:, chunk(i)] = xt[:, chunk(i)] - dot3(halves(tw[1]), halves(y2b[chunk(i), :]), NT)
 
     def apply(p, n):
-        tw[p] = dot3(halves(tb[p]), halves(wf[n]), NT)
+        tw[p] = dot3(halves(wf[n]), halves(tb[p]), NT)
 
     def raw(i):
         wait_y(0, i)
         first = halves(y1b[chunk(i), :])
-        w[1] += dot3(halves(xb[chunk(i), :]), first, TN)
+        w[1] += dot3(halves(xt[:, chunk(i)]), first, NN)
         gram[...] += dot3(halves(y2b[chunk(i), :]), first, TN)
 
     def rest():
@@ -251,14 +273,14 @@
     sent = all_sum(0, lambda: None, rest, nearly, lambda: pass_on(0, nq - 1))
     apply(1, 0)
     raw(nq - 1)
-    w[1] = w[1] - dot3(halves(tw[1]), halves(gram[...]), TN)
+    w[1] = w[1] - dot3(halves(tw[1]), halves(gram[...]), NN)
 
     def take_extra(i):
         pass_on(1, i)
         pass_on(0, i)
 
     def extra_inner(i):
-        wait_x(i)
+        turn(i)
         wait_y(1, i)
         inner(i)
 
@@ -270,26 +292,40 @@
         1, lambda: loop(0, nq, inner), lambda: loop(nq + early, held, send_bulk), lambda: None, early_extra)
     apply(0, 1)
 
-    def v_mate(i):
-        block = vb.at[k, chunk(i)]
-        return send(block, block, vm_s.at[i], vm_r.at[i], mate)
-
-    def v_peer(i):
-        return send(vb.at[k, chunk(i)], vb.at[k, chunk(i + nq)], vp_s.at[i], vp_r.at[i], peer)
+    def columns(g):
+        return pl.ds(g * span, span)
+
+    def v_mate(g, i):
+        block = vt.at[k, columns(g), chunk(i)]
+        return send(block, block, vm_s.at[g, i], vm_r.at[g, i], mate)
+
+    def v_peer(g, i):
+        return send(
+            vt.at[k, columns(g), chunk(i)], vt.at[k, columns(g), chunk(i + nq)], vp_s.at[g, i], vp_r.at[g, i], peer)
 
     def v_out(i):
-        return pltpu.make_async_copy(vb.at[k, chunk(i), lanes(x)], vec_hbm.at[place(i, x)], vo.at[i])
+        return pltpu.make_async_copy(vst.at[chunk(i)], vec_hbm.at[place(i, x)], vo.at[i])
+
+    def write_out(i):
+        for side in range(2):
+            @pl.when(x == side)
+            def _():
+                block = [None] * (bw // part)
+                for src, dst in pieces(0, side):
+                    block[src // part] = vt[k, dst : dst + part, chunk(i)]
+                vst[chunk(i), :] = jnp.concatenate(block, axis=0).T
+        v_out(i).start()
 
     def finish(i):
-        vb[k, chunk(i), :] = xb[chunk(i), :] - dot3(halves(y1b[chunk(i), :]), halves(tw[0]), NN)
+        vt[k, :, chunk(i)] = xt[:, chunk(i)] - dot3(halves(tw[0]), halves(y1b[chunk(i), :]), NT)
 
     def ship(i):
-        v_mate(i).start()
-        v_out(i).start()
+        for g in range(groups):
+            v_mate(g, i).start()
 
     def finish_sent(i):
         finish(i)
-        v_peer(i).start()
+        v_peer(0, i).start()
         ship(i)
 
     def finish_kept(i):
@@ -302,36 +338,52 @@
         ship(i)
 
     loop(extra, nq, finish_sent)
+    for g in range(1, groups):
+        loop(extra, nq, lambda i: v_peer(g, i).start())
     loop(nq + early, held, take_extra)
     loop(0, extra, finish_kept)
     loop(nq + early, held, extra_inner)
     loop(nq, held, finish_extra)
 
-    def columns(i):
-        return halves(sb[:, place(i, x)])
-
     def multiply(i):
-        v_mate(i).wait_recv()
-        part = columns(i)
+        for g in range(groups):
+            v_mate(g, i).wait_recv()
+        right = halves(sb[:, place(i, x)])
         for h in range(2):
-            pacc[h] += dot3(part, halves(vb[h, chunk(i), :]), NN)
-
-    def multiply_far(i):
-        v_peer(i - nq).wait_recv()
-        ship(i)
-        part = columns(i)
-        pacc[k] += dot3(part, halves(vb[k, chunk(i), :]), NN)
-        v_mate(i).wait_recv()
-        pacc[1 - k] += dot3(part, halves(vb[1 - k, chunk(i), :]), NN)
+            added = dot3(halves(vt[h, :, chunk(i)]), right, NT)
+            for g in range(groups):
+                pt[g, h] += added[g * span : (g + 1) * span]
+
+    def multiply_far(g, i):
+        v_peer(g, i - nq).wait_recv()
+        v_mate(g, i).start()
+        right = halves(sb[:, place(i, x)])
+        pt[g, k] += dot3(halves(vt[k, columns(g), chunk(i)]), right, NT)
+        v_mate(g, i).wait_recv()
+        pt[g, 1 - k] += dot3(halves(vt[1 - k, columns(g), chunk(i)]), right, NT)
+
+    def scatter(g):
+        def piece(zz, yy):
+            return pt.at[g, lax.rem(zz, 2), aligned((zz // 2) * 2 + yy, part)]
+
+        return Sum(2 + g, piece, pyb.at[g], pzb.at[g])
+
+    def collect(g):
+        out_ref[g * part : (g + 1) * part, :] = last[g].total()
 
     loop(0, held, multiply)
-    loop(held, 2 * nq, multiply_far)
-
-    for h in range(2):
-        for side in range(2):
-            pt[h + 2 * side] = pacc[h, :, side * bw : (side + 1) * bw].T
-
-    share = out_ref.shape[0]
+    loop(0, held, write_out)
+    last = []
+    for g in range(groups):
+        for i in range(held, 2 * nq):
+            multiply_far(g, i)
+            if g and i == held:
+                last[g - 1].relay()
+        if g and held == 2 * nq:
+            last[g - 1].relay()
+        last.append(scatter(g))
+        if g:
+            collect(g - 1)
 
     def drain(i):
         x_peer(i).wait_send()
@@ -341,23 +393,25 @@
             y_forward(p, i).wait_send()
 
     def drain_v(i):
-        v_mate(i).wait_send()
+        for g in range(groups):
+            v_mate(g, i).wait_send()
         v_out(i).wait()
 
-    def drain_all():
-        for copy in sent:
-            copy.wait_send()
-        loop(0, held, drain)
-        loop(extra, nq, lambda i: v_peer(i).wait_send())
-        loop(0, 2 * nq, drain_v)
-
-    total, last = sum_rows(2, lambda zz, yy: pt.at[zz, aligned(yy, share)], pyb, pzb, drain_all)
-    out_ref[...] = total
-    for copy in last:
+    last[-1].relay()
+    loop(held, 2 * nq, write_out)
+    for copy in sent:
         copy.wait_send()
+    loop(0, held, drain)
+    for g in range(groups):
+        loop(extra, nq, lambda i: v_peer(g, i).wait_send())
+    loop(0, 2 * nq, drain_v)
+    collect(groups - 1)
+    for done in last:
+        done.wait_sends()
 
 
 CHUNK = 512
+GROUPS = 2
 AHEAD = 3
 EARLY, LATE = 1, 1
 
@@ -370,14 +424,15 @@
     q = min(CHUNK, half)
     nq = half // q
     early, late = min(EARLY, nq), min(LATE, nq - min(EARLY, nq))
-    extra = early + late
-    held = nq + extra
+    held = nq + early + late
     kept = held * q
     wide = 2 * bw
     f32 = jnp.float32
     rows = wide // nrow
     mine = slab.shape[0]
     share = ncol * bw // nrow
+    g = GROUPS
+    part = share // g
     sem = pltpu.SemaphoreType.DMA
     vmem = pltpu.VMEM
     vectors, product = pl.pallas_call(
@@ -386,29 +441,33 @@
             jax.ShapeDtypeStruct((size, bw), f32),
             jax.ShapeDtypeStruct((share, mine), f32),
         ),
-        in_specs=[pl.BlockSpec(memory_space=pl.ANY)] * 4,
+        in_specs=[pl.BlockSpec(memory_space=pltpu.HBM)] * 4,
         out_specs=(pl.BlockSpec(memory_space=pl.ANY), pl.BlockSpec(memory_space=pltpu.VMEM)),
         scratch_shapes=[
-            vmem((kept, wide), f32), vmem((kept, panel), f32), vmem((kept, panel), f32),
-            vmem(slab.shape, f32), vmem(factors.shape, f32), vmem((2, size, wide), f32),
-            vmem((2, wide, panel), f32), vmem((panel, panel), f32), vmem((2, wide, panel), f32), vmem((2, panel, wide), f32),
+            vmem((kept, wide), f32), vmem((wide, kept), f32), vmem((kept, panel), f32), vmem((kept, panel), f32),
+            vmem(slab.shape, f32), vmem(factors.shape, f32), vmem((2, wide, size), f32), vmem((size, bw), f32),
+            vmem((2, wide, panel), f32), vmem((panel, panel), f32),
+            vmem((2, wide, panel), f32), vmem((2, wide, panel), f32),
             vmem((2, nz, rows, panel), f32), vmem((2, nz, rows, panel), f32),
             vmem((2, rows, panel), f32), vmem((2, rows, panel), f32),
-            vmem((2, mine, wide), f32), vmem((nz, bw, mine), f32),
-            vmem((nz, share, mine), f32), vmem((nz, share, mine), f32),
+            vmem((g, 2, wide // g, mine), f32),
+            vmem((g, nz, part, mine), f32), vmem((g, nz, part, mine), f32),
             sem((held,)), sem((2, held)), sem((2,)),
             sem((held,)), sem((held,)), sem((2, held)), sem((2, held)),
             sem((2, held)), sem((2, held)), sem((2, held)), sem((2, held)),
-            sem((3, nz)), sem((3, nz)), sem((3, nz)), sem((3, nz)),
+            sem((2 + g, nz)), sem((2 + g, nz)), sem((2 + g, nz)), sem((2 + g, nz)),
             sem((2,)), sem((2,)),
             sem((2, nz)), sem((2, nz)), sem((2, nz)), sem((2, nz)),
-            sem((nq,)), sem((nq,)), sem((2 * nq,)), sem((2 * nq,)), sem((2 * nq,)),
+            sem((g, nq)), sem((g, nq)), sem((g, 2 * nq)), sem((g, 2 * nq)), sem((2 * nq,)),
         ],
         compiler_params=pltpu.CompilerParams(
-            collective_id=0, has_side_effects=True, vmem_limit_bytes=66_000_000),
+            collective_id=0, has_side_effects=True, vmem_limit_bytes=VMEM_BYTES),
         name="whole",
     )(eigvecs, reflectors, factors, slab)
     return vectors, product.T
+
+
+VMEM_BYTES = 52_000_000
 
 
 def on_any(nrow, ncol, eigvecs, reflectors, factors, slab):

time: 163 us -> 157 us (0.963)
  Pallas kernels: 157 us -> 152 us
    pallas_call x1, Pallas kernels: 157 us -> 152 us  [on_grid(): pl.pallas_call(functools.partial(whole_kernel, (nz, q, nq, min(AHEAD, nq)...]
where the time goes in v2:
time: 157 us; the launch traced here: 156 us
  Pallas kernels  152 us (97%)
  local copies, waits for them, and re-layouts  3.56 us (2%)
    pallas_call x1, Pallas kernels, on_grid(): pl.pallas_call(functools.partial(whole_kernel, (nz, q, nq, min(AHEAD, nq)...  152 us
    unnamed x4, local copies, waits for them, and re-layouts  3.56 us

profile of v2, /device:TPU:0, one launch (start us, length us, event | category | flops | bytes accessed | tf_op | source)
XLA Modules:
  0.0 156.5 jit_solution(3594256801012948976)
XLA Ops:
  0.6 0.0 copy-start
  0.6 1.6 %copy-done = f32[4096,128]{1,0:T(8,128)S(1)} copy-done((f32[4096,128]{1,0:T(8,128)S(1)}, f32[4096,128]{1,0:T(8,128)}, u32[]{:S(2)}) %copy-start) | copy-done | bytes 2097176
  2.2 152.3 %whole.1 = (f32[4096,128]{1,0:T(8,128)S(1)}, f32[64,512]{1,0:T(8,128)S(1)}) custom-call(f32[4096,128]{1,0:T(8,128)S(1)} %copy-done, f32[2,4096,128]{2,1,0:T(8,128)} %y_hbm.1, f32[2,512,512]{2,1,0:T(8,128)} %t_hbm.1, f32[512,4096]{1,0:T(8,128)} %s_hbm.1), custom_call_target="tpu_custom_call" | custom-call | tf_op jit(solution)/shard_map/whole/pallas_call | solution.py:438
  154.5 1.3 copy.8
  155.8 0.7 copy.9
Async XLA Ops:
  0.6 1.6 %copy-start = (f32[4096,128]{1,0:T(8,128)S(1)}, f32[4096,128]{1,0:T(8,128)}, u32[]{:S(2)}) copy-start(f32[4096,128]{1,0:T(8,128)} %x_hbm.1) | copy-start | bytes 6291460

commit v3 on v0

v3 whole, which is shorter than its diff:
```python
import functools

import jax
import jax.numpy as jnp
from jax import lax
from jax.experimental import pallas as pl
from jax.experimental.pallas import tpu as pltpu
from jax.sharding import PartitionSpec as P

MESH = pl.DeviceIdType.MESH
NN = ((1,), (0,))
NT = ((1,), (1,))
TN = ((0,), (0,))


def dot(left, right, dims=NN):
    return lax.dot_general(
        left, right, (dims, ((), ())), precision=lax.Precision.HIGH, preferred_element_type=jnp.float32
    )


def tdot(left, right):
    return dot(left, right, TN)


def halves(a):
    high = a.astype(jnp.bfloat16)
    return high, (a - high.astype(jnp.float32)).astype(jnp.bfloat16)


def dot3(left, right, dims):
    def one(a, b):
        return lax.dot_general(a, b, (dims, ((), ())), preferred_element_type=jnp.float32)

    (lh, ll), (rh, rl) = left, right
    return one(lh, rh) + (one(lh, rl) + one(ll, rh))


def whole_kernel(
    plan, x_hbm, y_hbm, t_hbm, s_hbm, vec_hbm, out_ref,
    xb, xt, y1b, y2b, sb, far_h, far_l, tb, vt, vst, w, gram, wf, tw, ybuf, zbuf, xs, xr, pt, pyb, pzb,
    ls, bulk_s, x_r, y_r, py_r, ry_r, rz_r, r_s, rx_s, rx_r, gz_r, gy_r, g_s, vp_r, vm_r, v_s,
):
    nz, q, nq, ahead, early, late, kept, sent, parts = plan
    half = nq * q
    must = [(i * q, q) for i in range(nq)]
    extras = early + late
    held = half + sum(n for _, n in extras)
    bw = x_hbm.shape[1]
    share = out_ref.shape[0]
    per = bw // share
    offs = [sum(parts[:g]) for g in range(len(parts))]
    spans = [(2 * per * o, 2 * per * n) for o, n in zip(offs, parts)]
    first_span = spans[0][1]
    wide = xt.shape[0]
    r, c = lax.axis_index("row"), lax.axis_index("col")
    z, y = r // 2, lax.rem(r, 2)
    x, k = c // 2, lax.rem(c, 2)
    mate = (r, c + 1 - 2 * k)
    peer = (r, c + 2 - 4 * x)
    peer_block = c + 2 - 4 * x
    ynext = (r + 1 - 2 * y, c)

    def zat(d):
        return lax.rem(z + d, nz)

    def znext(d):
        return (zat(d) * 2 + y, c)

    partners = [mate, peer, ynext] + [znext(d) for d in range(1, nz)]
    barrier = pltpu.get_barrier_semaphore()
    for other in partners:
        pl.semaphore_signal(barrier, inc=1, device_id=other, device_id_type=MESH)
    pl.semaphore_wait(barrier, len(partners))

    def send(src, dst, s, t, device):
        return pltpu.make_async_remote_copy(src, dst, s, t, device_id=device, device_id_type=MESH)

    def sent_all(ref, s):
        send(ref, ref, s, s, mate).wait_send()

    def at(m):
        return pl.ds(m[0], m[1])

    def place(m, side):
        start, size = m
        base = side * half + start if start < half else (1 - side) * half + start - half
        return pl.ds(pl.multiple_of(base, 128), size)

    def lanes(b):
        return pl.ds(pl.multiple_of(b * bw, bw), bw)

    def index(m):
        return m[0] // q if m[0] < half else nq + extras.index(m)

    panels = (y1b, y2b)

    def x_local(m):
        return pltpu.make_async_copy(x_hbm.at[place(m, x)], xb.at[at(m), lanes(x)], x_r.at[index(m)])

    def x_peer(m):
        return send(x_hbm.at[place(m, 1 - x)], xb.at[at(m), lanes(x)], bulk_s.at[0], x_r.at[index(m)], peer)

    def y_local(p, m):
        return pltpu.make_async_copy(
            y_hbm.at[p, place(m, x)], panels[p].at[at(m), lanes(c)], y_r.at[p, index(m)])

    def y_peer(p, m):
        return send(
            y_hbm.at[p, place(m, 1 - x)], panels[p].at[at(m), lanes(c)], bulk_s.at[1], py_r.at[p, index(m)], peer)

    def y_mate(p, m):
        return send(
            y_hbm.at[p, place(m, x)], panels[p].at[at(m), lanes(c)], bulk_s.at[2], y_r.at[p, index(m)], mate)

    def y_forward(p, m):
        block = panels[p].at[at(m), lanes(peer_block)]
        return send(block, block, bulk_s.at[3], y_r.at[p, index(m)], mate)

    def wait_y(p, m):
        block = panels[p].at[at(m), pl.ds(0, 3 * bw)]
        pltpu.make_async_copy(block, block, y_r.at[p, index(m)]).wait()

    def pass_on(p, m):
        y_peer(p, m).wait_recv()
        y_forward(p, m).start()

    def send_bulk(m):
        x_peer(m).start()
        y_peer(1, m).start()
        y_peer(0, m).start()

    for m in must:
        x_peer(m).start()
        y_peer(1, m).start()
    for m in must[:ahead]:
        y_peer(0, m).start()
    for m in must + extras:
        x_local(m).start()
        for p in (1, 0):
            y_mate(p, m).start()
            y_local(p, m).start()
    t_copy = pltpu.make_async_copy(t_hbm, tb, ls.at[0])
    s_copy = pltpu.make_async_copy(s_hbm, sb, ls.at[1])
    t_copy.start()
    s_copy.start()

    w[...] = jnp.zeros_like(w)
    gram[...] = jnp.zeros_like(gram)
    pt[...] = jnp.zeros_like(pt)
    t_copy.wait()
    s_copy.wait()
    far = [(start + half, size) for start, size in sent]
    reach = far[0][0]
    for m in far:
        high, low = halves(sb[:, place(m, x)])
        far_h[:, m[0] - reach : m[0] - reach + m[1]] = high
        far_l[:, m[0] - reach : m[0] - reach + m[1]] = low

    def pieces(block, side):
        for o, n, (base, _) in zip(offs, parts, spans):
            for h in range(per):
                yield block + h * share + o, base + (side * per + h) * n, n

    def turn(m):
        pltpu.make_async_copy(xb.at[at(m)], xb.at[at(m)], x_r.at[index(m)]).wait()
        turned = xb[at(m), :].T
        for side in range(2):
            for src, dst, n in pieces(side * bw, side):
                xt[dst : dst + n, at(m)] = turned[src : src + n]

    def begin(m):
        turn(m)
        wait_y(1, m)
        w[0] += dot3(halves(xt[:, at(m)]), halves(y2b[at(m), :]), NN)

    for i, m in enumerate(must):
        pass_on(1, m)
        if i:
            begin(must[i - 1])
    begin(must[-1])

    class Sum:
        def __init__(self, n, piece, ys, zs, whole):
            self.n, self.piece, self.ys, self.zs, self.whole = n, piece, ys, zs, whole
            self.order = list(range(1, nz)) + [0]
            self.out = [
                send(piece(zat(d), 1 - y), ys(d), r_s.at[n], ry_r.at[n, d], ynext) for d in self.order]
            self.hops = [send(piece(zat(d), y), zs(d), r_s.at[n], rz_r.at[n, d], znext(d)) for d in range(1, nz)]
            for copy in self.out:
                copy.start()

        def relay(self):
            for d, copy in zip(self.order, self.out):
                copy.wait_recv()
                if d:
                    self.piece(zat(d), y)[...] += self.ys(d)[...]
                    self.hops[d - 1].start()

        def total(self):
            total = self.piece(z, y)[...] + self.ys(0)[...]
            for d in range(1, nz):
                self.hops[d - 1].wait_recv()
                total = total + self.zs(d)[...]
            return total

        def drain(self):
            sent_all(self.whole, r_s.at[self.n])

    class AllSum:
        def __init__(self, n, panel, base, size):
            self.n = n
            rows = size // (2 * nz)
            self.rows = pl.ds(base // (2 * nz), rows)

            def block(ref, zz, yy):
                return ref.at[panel, pl.ds(pl.multiple_of(base + (zz * 2 + yy) * rows, 8), rows)]

            self.final = lambda zz, yy: block(wf, zz, yy)
            self.whole = w.at[panel, pl.ds(0, (2 * nz - 1) * rows)]
            self.panel = panel
            self.sum = Sum(
                n, lambda zz, yy: block(w, zz, yy),
                lambda d: ybuf.at[panel, d, self.rows], lambda d: zbuf.at[panel, d, self.rows], self.whole)
            self.relay = self.sum.relay

        def swap(self):
            n = self.n
            mine, other = xs.at[self.panel, self.rows], xr.at[self.panel, self.rows]
            mine[...] = self.sum.total()
            self.swapped = send(mine, other, rx_s.at[n], rx_r.at[n], peer)
            self.swapped.start()

        def gather(self):
            n = self.n
            self.swapped.wait_recv()
            mine = self.final(z, y)
            mine[...] = xs[self.panel, self.rows] + xr[self.panel, self.rows]
            self.along = [send(mine, mine, g_s.at[n], gz_r.at[n, d], znext(d)) for d in range(1, nz)]
            for copy in self.along:
                copy.start()
            self.across = [send(mine, mine, g_s.at[n], gy_r.at[n, 0], ynext)]
            self.across[0].start()

        def forward(self):
            for d in range(1, nz):
                self.along[d - 1].wait_recv()
                block = self.final(lax.rem(z + nz - d, nz), y)
                self.across.append(send(block, block, g_s.at[self.n], gy_r.at[self.n, d], ynext))
                self.across[-1].start()

        def finish(self):
            for copy in self.across:
                copy.wait_recv()

        def drain(self):
            self.sum.drain()
            self.swapped.wait_send()
            sent_all(self.whole, g_s.at[self.n])

    def inner(m):
        xt[:, at(m)] = xt[:, at(m)] - dot3(halves(tw[1]), halves(y2b[at(m), :]), NT)

    def raw(m):
        wait_y(0, m)
        first = halves(y1b[at(m), :])
        w[1] += dot3(halves(xt[:, at(m)]), first, NN)
        gram[...] += dot3(halves(y2b[at(m), :]), first, TN)

    a0 = AllSum(0, 0, 0, wide)
    a0.relay()
    a0.swap()
    for m in must[ahead:]:
        y_peer(0, m).start()
    for m in early:
        send_bulk(m)
    for m in must[:-2]:
        pass_on(0, m)
    for m in must[:-2]:
        raw(m)
    a0.gather()
    pass_on(0, must[-2])
    raw(must[-2])
    a0.forward()
    pass_on(0, must[-1])
    a0.finish()
    tw[1] = dot3(halves(wf[0]), halves(tb[1]), NT)
    raw(must[-1])
    w[1] = w[1] - dot3(halves(tw[1]), halves(gram[...]), NN)

    def take(m):
        pass_on(1, m)
        pass_on(0, m)

    def extra_inner(m):
        turn(m)
        wait_y(1, m)
        inner(m)

    a1 = AllSum(1, 1, 0, first_span)
    a2 = AllSum(2, 1, first_span, wide - first_span)
    a1.relay()
    a2.relay()
    for m in must:
        inner(m)
    a1.swap()
    a2.swap()
    for m in late:
        send_bulk(m)
    a1.gather()
    a2.gather()
    a1.forward()
    a2.forward()
    for m in early:
        take(m)
    for m in early:
        extra_inner(m)

    def band(g):
        return pl.ds(*spans[g])

    later = pl.ds(first_span, wide - first_span)
    locals_ = sent + kept + extras

    def v_mate(b, rows, m):
        block = vt.at[k, rows, at(m)]
        slot = locals_.index(m) if m in locals_ else len(locals_) + far.index(m)
        return send(block, block, v_s.at[1], vm_r.at[b, slot], mate)

    def v_peer(g, j):
        return send(vt.at[k, band(g), at(sent[j])], vt.at[k, band(g), at(far[j])], v_s.at[0], vp_r.at[g, j], peer)

    def v_out(m):
        return pltpu.make_async_copy(vst.at[at(m)], vec_hbm.at[place(m, x)], v_s.at[2])

    def write_out(m):
        for side in range(2):
            @pl.when(x == side)
            def _():
                block = [vt[k, dst : dst + n, at(m)] for _, dst, n in sorted(pieces(0, side))]
                vst[at(m), :] = jnp.concatenate(block, axis=0).T
        v_out(m).start()

    def weigh(rows):
        tw[0, rows, :] = dot3(halves(wf[1, rows, :]), halves(tb[0]), NT)

    def finish(rows, m):
        vt[k, rows, at(m)] = xt[rows, at(m)] - dot3(halves(tw[0, rows, :]), halves(y1b[at(m), :]), NT)

    a1.finish()
    weigh(band(0))
    for j, m in enumerate(sent):
        finish(band(0), m)
        v_peer(0, j).start()
    a2.finish()
    weigh(later)
    for j, m in enumerate(sent):
        finish(later, m)
        v_peer(1, j).start()
    for g in range(2, len(parts)):
        for j in range(len(sent)):
            v_peer(g, j).start()
    everything = pl.ds(0, wide)
    for m in sent:
        v_mate(0, everything, m).start()
    for m in kept:
        finish(everything, m)
        v_mate(0, everything, m).start()
    for m in late:
        take(m)
    for m in early:
        wait_y(0, m)
        finish(everything, m)
        v_mate(0, everything, m).start()

    def multiply(m):
        v_mate(0, everything, m).wait_recv()
        right = halves(sb[:, place(m, x)])
        for h in range(2):
            pt[h] += dot3(halves(vt[h, :, at(m)]), right, NT)

    for m in sent + kept:
        multiply(m)
    for m in late:
        extra_inner(m)
        wait_y(0, m)
        finish(everything, m)
        v_mate(0, everything, m).start()
    for m in extras:
        multiply(m)
    for m in locals_:
        write_out(m)

    def multiply_far(g, j, h):
        m = far[j]
        cut = slice(m[0] - reach, m[0] - reach + m[1])
        right = far_h[:, cut], far_l[:, cut]
        pt[h, band(g), :] += dot3(halves(vt[h, band(g), at(m)]), right, NT)

    def scatter(g):
        n = parts[g]

        def piece(zz, yy):
            start = spans[g][0] + ((zz // 2) * per + yy) * n
            return pt.at[lax.rem(zz, 2), pl.ds(pl.multiple_of(start, 8), n)]

        def rows(ref):
            return lambda d: ref.at[d, pl.ds(offs[g], n)]

        return Sum(3 + g, piece, rows(pyb), rows(pzb), pt.at[0, pl.ds(0, (2 * nz - 1) * n)])

    def collect(g):
        out_ref[offs[g] : offs[g] + parts[g], :] = last[g].total()

    last = []
    todo = [(g, j) for g in range(len(parts)) for j in range(len(sent))]

    def mate_half(g, j):
        v_mate(g, band(g), far[j]).wait_recv()
        multiply_far(g, j, 1 - k)
        if j == len(sent) - 1:
            last.append(scatter(g))
        elif g and j == 0:
            last[g - 1].relay()

    for t, (g, j) in enumerate(todo):
        v_peer(g, j).wait_recv()
        v_mate(g, band(g), far[j]).start()
        multiply_far(g, j, k)
        if t:
            mate_half(*todo[t - 1])
    mate_half(*todo[-1])
    for g in range(len(parts) - 1):
        collect(g)
    last[-1].relay()
    for m in far:
        write_out(m)
    for s in (a0, a1, a2):
        s.drain()
    sent_all(x_hbm.at[pl.ds(0, held)], bulk_s.at[0])
    for i in (1, 2, 3):
        sent_all(y_hbm.at[:, pl.ds(0, held)], bulk_s.at[i])
    sent_all(vt.at[0, :, pl.ds(0, sum(n for _, n in sent))], v_s.at[0])
    sent_all(vt.at[0], v_s.at[1])
    pltpu.make_async_copy(vst, vec_hbm, v_s.at[2]).wait()
    collect(len(parts) - 1)
    for done in last:
        done.drain()


CHUNK = 4
AHEAD = 3
EARLY = (3,)
LATE = (2,)
PARTS = (4, 2, 2)
UNITS = 16
VMEM_BYTES = 54_000_000


def on_grid(nrow, ncol, eigvecs, reflectors, factors, slab):
    size, bw = eigvecs.shape
    panel = factors.shape[1]
    nz = nrow // 2
    half = size // 2
    unit = half // UNITS
    q = CHUNK * unit
    nq = half // q

    def ranges(start, sizes):
        out = []
        for n in sizes:
            out.append((start, n * unit))
            start += n * unit
        return out

    early = ranges(half, EARLY)
    late = ranges(half + sum(n for _, n in early), LATE)
    extra = sum(EARLY) + sum(LATE)
    kept = ranges(0, (extra,))
    first = (UNITS - extra) % CHUNK
    sent = ranges(extra * unit, ((first,) if first else ()) + (CHUNK,) * ((UNITS - extra) // CHUNK))
    held = half + extra * unit
    away = half - extra * unit
    wide = 2 * bw
    f32 = jnp.float32
    rows = wide // nrow
    mine = slab.shape[0]
    share = ncol * bw // nrow
    parts = tuple(n * share // sum(PARTS) for n in PARTS)
    g = len(parts)
    chunks = nq + len(EARLY) + len(LATE)
    slots = 2 * len(sent) + len(kept) + len(EARLY) + len(LATE)
    sem = pltpu.SemaphoreType.DMA
    vmem = pltpu.VMEM
    vectors, product = pl.pallas_call(
        functools.partial(whole_kernel, (nz, q, nq, AHEAD, early, late, kept, sent, parts)),
        out_shape=(
            jax.ShapeDtypeStruct((size, bw), f32),
            jax.ShapeDtypeStruct((share, mine), f32),
        ),
        in_specs=[pl.BlockSpec(memory_space=pltpu.HBM)] * 4,
        out_specs=(pl.BlockSpec(memory_space=pl.ANY), pl.BlockSpec(memory_space=pltpu.VMEM)),
        scratch_shapes=[
            vmem((held, wide), f32), vmem((wide, held), f32), vmem((held, panel), f32), vmem((held, panel), f32),
            vmem(slab.shape, f32), vmem((mine, away), jnp.bfloat16), vmem((mine, away), jnp.bfloat16),
            vmem(factors.shape, f32), vmem((2, wide, size), f32), vmem((size, bw), f32),
            vmem((2, wide, panel), f32), vmem((panel, panel), f32),
            vmem((2, wide, panel), f32), vmem((2, wide, panel), f32),
            vmem((2, nz, rows, panel), f32), vmem((2, nz, rows, panel), f32),
            vmem((2, rows, panel), f32), vmem((2, rows, panel), f32),
            vmem((2, wide, mine), f32),
            vmem((nz, share, mine), f32), vmem((nz, share, mine), f32),
            sem((2,)), sem((4,)), sem((chunks,)), sem((2, chunks)), sem((2, chunks)),
            sem((3 + g, nz)), sem((3 + g, nz)), sem((3 + g,)), sem((3,)), sem((3,)),
            sem((3, nz)), sem((3, nz)), sem((3,)), sem((g, len(sent))), sem((g, slots)), sem((3,)),
        ],
        compiler_params=pltpu.CompilerParams(
            collective_id=0, has_side_effects=True, vmem_limit_bytes=VMEM_BYTES),
        name="whole",
    )(eigvecs, reflectors, factors, slab)
    return vectors, product.T


def on_any(nrow, ncol, eigvecs, reflectors, factors, slab):
    c = lax.axis_index("col")
    first_own, second_own = reflectors[0], reflectors[1]
    all_x, second_y, first_y = (
        lax.all_gather(block, "col", axis=1, tiled=True) for block in (eigvecs, second_own, first_own)
    )
    own = second_own.shape[1]
    both = jnp.concatenate([second_own, first_own], axis=1)
    stacked = jnp.concatenate([tdot(both, all_x), tdot(first_own, second_y)])
    slab_x, slab_second, slab_first = (dot(block, slab, ((0,), (1,))) for block in (all_x, second_y, first_y))
    sums = lax.all_gather(lax.psum(stacked, "row"), "col")
    panel = factors.shape[1]
    second_w, first_raw, gram = (sums[:, i * own : (i + 1) * own].reshape(panel, -1) for i in range(3))
    second_tw = dot(factors[1], second_w)
    first_tw = dot(factors[0], first_raw - dot(gram, second_tw))
    partial = slab_x - tdot(second_tw, slab_second) - tdot(first_tw, slab_first)
    product = lax.psum_scatter(partial, "row", tiled=True)
    vectors = eigvecs
    for block, tw in ((second_y, second_tw), (first_y, first_tw)):
        width = eigvecs.shape[1]
        vectors = vectors - dot(block, lax.dynamic_slice_in_dim(tw, c * width, width, axis=1))
    return vectors, product.T


def solution(mesh):
    nrow, ncol = mesh.shape["row"], mesh.shape["col"]
    fits = ncol == 4 and nrow == 2 * ncol
    return jax.shard_map(
        functools.partial(on_grid if fits else on_any, nrow, ncol),
        mesh=mesh,
        in_specs=(P("row", "col"), P(None, "row", "col"), P(), P("col", "row")),
        out_specs=(P("row", "col"), P("col", "row")),
        check_vma=False,
    )
```

time: 172 us -> 158 us (0.919)
  Pallas kernels: 167 us -> 156 us
  local copies, waits for them, and re-layouts: 3.74 us -> 1.98 us
    pallas_call x1, Pallas kernels: 167 us -> 156 us  [on_grid(): pl.pallas_call(functools.partial(whole_kernel, (nz, q, nq, AHEAD, early,...]
    unnamed x4 -> x2, local copies, waits for them, and re-layouts: 3.74 us -> 1.98 us
where the time goes in v3:
time: 158 us
  Pallas kernels  156 us (99%)
  local copies, waits for them, and re-layouts  1.98 us (1%)
    pallas_call x1, Pallas kernels, on_grid(): pl.pallas_call(functools.partial(whole_kernel, (nz, q, nq, AHEAD, early,...  156 us

profile of v3, /device:TPU:0, one launch (start us, length us, event | category | flops | bytes accessed | tf_op | source)
XLA Modules:
  0.0 158.2 jit_solution(16343011182225622802)
XLA Ops:
  0.6 155.6 %whole.1 = (f32[4096,128]{1,0:T(8,128)S(1)}, f32[64,512]{1,0:T(8,128)S(1)}) custom-call(f32[4096,128]{1,0:T(8,128)} %x_hbm.1, f32[2,4096,128]{2,1,0:T(8,128)} %y_hbm.1, f32[2,512,512]{2,1,0:T(8,128)} %t_hbm.1, f32[512,4096]{1,0:T(8,128)} %s_hbm.1), custom_call_target="tpu_custom_call" | custom-call | tf_op jit(solution)/shard_map/whole/pallas_call | solution.py:495
  156.2 1.3 copy.8
  157.6 0.7 copy.9

commit v4 on v3

--- a/solution.py
+++ b/solution.py
@@ -79,6 +79,9 @@
     def sent_all(ref, s):
         send(ref, ref, s, s, mate).wait_send()
 
+    def arrive(ref, s):
+        send(ref, ref, s, s, mate).wait_recv()
+
     def at(m):
         return pl.ds(m[0], m[1])
 
@@ -183,29 +186,30 @@
     class Sum:
         def __init__(self, n, piece, ys, zs, whole):
             self.n, self.piece, self.ys, self.zs, self.whole = n, piece, ys, zs, whole
-            self.order = list(range(1, nz)) + [0]
+            self.pending = list(range(1, nz))
             self.out = [
-                send(piece(zat(d), 1 - y), ys(d), r_s.at[n], ry_r.at[n, d], ynext) for d in self.order]
-            self.hops = [send(piece(zat(d), y), zs(d), r_s.at[n], rz_r.at[n, d], znext(d)) for d in range(1, nz)]
+                send(piece(zat(d), 1 - y), ys(d), r_s.at[n], ry_r.at[n, d], ynext) for d in self.pending + [0]]
+            self.hops = [send(piece(zat(d), y), zs(d), r_s.at[n], rz_r.at[n], znext(d)) for d in range(1, nz)]
             for copy in self.out:
                 copy.start()
 
-        def relay(self):
-            for d, copy in zip(self.order, self.out):
-                copy.wait_recv()
-                if d:
-                    self.piece(zat(d), y)[...] += self.ys(d)[...]
-                    self.hops[d - 1].start()
+        def relay(self, count=nz):
+            for d in self.pending[:count]:
+                self.out[d - 1].wait_recv()
+                self.piece(zat(d), y)[...] += self.ys(d)[...]
+                self.hops[d - 1].start()
+            self.pending = self.pending[count:]
 
         def total(self):
+            self.out[-1].wait_recv()
             total = self.piece(z, y)[...] + self.ys(0)[...]
+            arrive(self.whole(nz - 1), rz_r.at[self.n])
             for d in range(1, nz):
-                self.hops[d - 1].wait_recv()
                 total = total + self.zs(d)[...]
             return total
 
         def drain(self):
-            sent_all(self.whole, r_s.at[self.n])
+            sent_all(self.whole(2 * nz - 1), r_s.at[self.n])
 
     class AllSum:
         def __init__(self, n, panel, base, size):
@@ -217,7 +221,7 @@
                 return ref.at[panel, pl.ds(pl.multiple_of(base + (zz * 2 + yy) * rows, 8), rows)]
 
             self.final = lambda zz, yy: block(wf, zz, yy)
-            self.whole = w.at[panel, pl.ds(0, (2 * nz - 1) * rows)]
+            self.whole = lambda count: w.at[panel, pl.ds(0, count * rows)]
             self.panel = panel
             self.sum = Sum(
                 n, lambda zz, yy: block(w, zz, yy),
@@ -239,24 +243,23 @@
             self.along = [send(mine, mine, g_s.at[n], gz_r.at[n, d], znext(d)) for d in range(1, nz)]
             for copy in self.along:
                 copy.start()
-            self.across = [send(mine, mine, g_s.at[n], gy_r.at[n, 0], ynext)]
+            self.across = [send(mine, mine, g_s.at[n], gy_r.at[n], ynext)]
             self.across[0].start()
 
         def forward(self):
             for d in range(1, nz):
                 self.along[d - 1].wait_recv()
                 block = self.final(lax.rem(z + nz - d, nz), y)
-                self.across.append(send(block, block, g_s.at[self.n], gy_r.at[self.n, d], ynext))
+                self.across.append(send(block, block, g_s.at[self.n], gy_r.at[self.n], ynext))
                 self.across[-1].start()
 
         def finish(self):
-            for copy in self.across:
-                copy.wait_recv()
+            arrive(self.whole(nz), gy_r.at[self.n])
 
         def drain(self):
             self.sum.drain()
             self.swapped.wait_send()
-            sent_all(self.whole, g_s.at[self.n])
+            sent_all(self.whole(2 * nz - 1), g_s.at[self.n])
 
     def inner(m):
         xt[:, at(m)] = xt[:, at(m)] - dot3(halves(tw[1]), halves(y2b[at(m), :]), NT)
@@ -283,9 +286,9 @@
     raw(must[-2])
     a0.forward()
     pass_on(0, must[-1])
+    raw(must[-1])
     a0.finish()
     tw[1] = dot3(halves(wf[0]), halves(tb[1]), NT)
-    raw(must[-1])
     w[1] = w[1] - dot3(halves(tw[1]), halves(gram[...]), NN)
 
     def take(m):
@@ -300,21 +303,21 @@
     a1 = AllSum(1, 1, 0, first_span)
     a2 = AllSum(2, 1, first_span, wide - first_span)
     a1.relay()
+    for m in must[:2]:
+        inner(m)
     a2.relay()
-    for m in must:
+    a1.swap()
+    for m in must[2:]:
         inner(m)
-    a1.swap()
     a2.swap()
     for m in late:
         send_bulk(m)
     a1.gather()
     a2.gather()
+    for m in early:
+        take(m)
     a1.forward()
     a2.forward()
-    for m in early:
-        take(m)
-    for m in early:
-        extra_inner(m)
 
     def band(g):
         return pl.ds(*spans[g])
@@ -324,8 +327,8 @@
 
     def v_mate(b, rows, m):
         block = vt.at[k, rows, at(m)]
-        slot = locals_.index(m) if m in locals_ else len(locals_) + far.index(m)
-        return send(block, block, v_s.at[1], vm_r.at[b, slot], mate)
+        slot = locals_.index(m) if m in locals_ else len(locals_) + b * len(far) + far.index(m)
+        return send(block, block, v_s.at[1], vm_r.at[slot], mate)
 
     def v_peer(g, j):
         return send(vt.at[k, band(g), at(sent[j])], vt.at[k, band(g), at(far[j])], v_s.at[0], vp_r.at[g, j], peer)
@@ -369,6 +372,7 @@
     for m in late:
         take(m)
     for m in early:
+        extra_inner(m)
         wait_y(0, m)
         finish(everything, m)
         v_mate(0, everything, m).start()
@@ -388,14 +392,13 @@
         v_mate(0, everything, m).start()
     for m in extras:
         multiply(m)
-    for m in locals_:
-        write_out(m)
-
-    def multiply_far(g, j, h):
+
+    def multiply_far(g, j):
         m = far[j]
         cut = slice(m[0] - reach, m[0] - reach + m[1])
-        right = far_h[:, cut], far_l[:, cut]
-        pt[h, band(g), :] += dot3(halves(vt[h, band(g), at(m)]), right, NT)
+        both = vt[:, band(g), at(m)].reshape(2 * spans[g][1], m[1])
+        added = dot3(halves(both), (far_h[:, cut], far_l[:, cut]), NT)
+        pt[:, band(g), :] += added.reshape(2, spans[g][1], pt.shape[2])
 
     def scatter(g):
         n = parts[g]
@@ -407,7 +410,7 @@
         def rows(ref):
             return lambda d: ref.at[d, pl.ds(offs[g], n)]
 
-        return Sum(3 + g, piece, rows(pyb), rows(pzb), pt.at[0, pl.ds(0, (2 * nz - 1) * n)])
+        return Sum(3 + g, piece, rows(pyb), rows(pzb), lambda count: sb.at[pl.ds(0, count * n), pl.ds(0, pt.shape[2])])
 
     def collect(g):
         out_ref[offs[g] : offs[g] + parts[g], :] = last[g].total()
@@ -415,26 +418,30 @@
     last = []
     todo = [(g, j) for g in range(len(parts)) for j in range(len(sent))]
 
-    def mate_half(g, j):
+    def arrived(g, j):
         v_mate(g, band(g), far[j]).wait_recv()
-        multiply_far(g, j, 1 - k)
+        multiply_far(g, j)
         if j == len(sent) - 1:
             last.append(scatter(g))
-        elif g and j == 0:
+        elif g and j == len(sent) - 2:
             last[g - 1].relay()
 
     for t, (g, j) in enumerate(todo):
         v_peer(g, j).wait_recv()
         v_mate(g, band(g), far[j]).start()
-        multiply_far(g, j, k)
         if t:
-            mate_half(*todo[t - 1])
-    mate_half(*todo[-1])
+            arrived(*todo[t - 1])
+        if t < len(locals_):
+            write_out(locals_[t])
+    arrived(*todo[-1])
+    for m in locals_[len(todo):]:
+        write_out(m)
+    for one in last:
+        one.relay()
+    for m in far:
+        write_out(m)
     for g in range(len(parts) - 1):
         collect(g)
-    last[-1].relay()
-    for m in far:
-        write_out(m)
     for s in (a0, a1, a2):
         s.drain()
     sent_all(x_hbm.at[pl.ds(0, held)], bulk_s.at[0])
@@ -452,7 +459,7 @@
 AHEAD = 3
 EARLY = (3,)
 LATE = (2,)
-PARTS = (4, 2, 2)
+PARTS = (2, 1, 1)
 UNITS = 16
 VMEM_BYTES = 54_000_000
 
@@ -489,7 +496,7 @@
     parts = tuple(n * share // sum(PARTS) for n in PARTS)
     g = len(parts)
     chunks = nq + len(EARLY) + len(LATE)
-    slots = 2 * len(sent) + len(kept) + len(EARLY) + len(LATE)
+    slots = (1 + g) * len(sent) + len(kept) + len(EARLY) + len(LATE)
     sem = pltpu.SemaphoreType.DMA
     vmem = pltpu.VMEM
     vectors, product = pl.pallas_call(
@@ -511,8 +518,8 @@
             vmem((2, wide, mine), f32),
             vmem((nz, share, mine), f32), vmem((nz, share, mine), f32),
             sem((2,)), sem((4,)), sem((chunks,)), sem((2, chunks)), sem((2, chunks)),
-            sem((3 + g, nz)), sem((3 + g, nz)), sem((3 + g,)), sem((3,)), sem((3,)),
-            sem((3, nz)), sem((3, nz)), sem((3,)), sem((g, len(sent))), sem((g, slots)), sem((3,)),
+            sem((3 + g, nz)), sem((3 + g,)), sem((3 + g,)), sem((3,)), sem((3,)),
+            sem((3, nz)), sem((3,)), sem((3,)), sem((g, len(sent))), sem((slots,)), sem((3,)),
         ],
         compiler_params=pltpu.CompilerParams(
             collective_id=0, has_side_effects=True, vmem_limit_bytes=VMEM_BYTES),

time: 158 us -> 147 us (0.930)
  Pallas kernels: 156 us -> 144 us
    pallas_call x1, Pallas kernels: 156 us -> 144 us  [on_grid(): pl.pallas_call(functools.partial(whole_kernel, (nz, q, nq, AHEAD, early,...]
where the time goes in v4:
time: 147 us
  Pallas kernels  144 us (98%)
  local copies, waits for them, and re-layouts  1.98 us (1%)
    pallas_call x1, Pallas kernels, on_grid(): pl.pallas_call(functools.partial(whole_kernel, (nz, q, nq, AHEAD, early,...  144 us

profile of v4, /device:TPU:0, one launch (start us, length us, event | category | flops | bytes accessed | tf_op | source)
XLA Modules:
  0.0 147.1 jit_solution(331456654874906701)
XLA Ops:
  0.6 144.5 %whole.1 = (f32[4096,128]{1,0:T(8,128)S(1)}, f32[64,512]{1,0:T(8,128)S(1)}) custom-call(f32[4096,128]{1,0:T(8,128)} %x_hbm.1, f32[2,4096,128]{2,1,0:T(8,128)} %y_hbm.1, f32[2,512,512]{2,1,0:T(8,128)} %t_hbm.1, f32[512,4096]{1,0:T(8,128)} %s_hbm.1), custom_call_target="tpu_custom_call" | custom-call | tf_op jit(solution)/shard_map/whole/pallas_call | solution.py:502
  145.1 1.3 copy.8
  146.4 0.7 copy.9

commit v5 on v4

--- a/solution.py
+++ b/solution.py
@@ -101,16 +101,16 @@
     def x_local(m):
         return pltpu.make_async_copy(x_hbm.at[place(m, x)], xb.at[at(m), lanes(x)], x_r.at[index(m)])
 
-    def x_peer(m):
-        return send(x_hbm.at[place(m, 1 - x)], xb.at[at(m), lanes(x)], bulk_s.at[0], x_r.at[index(m)], peer)
+    def x_peer(m, slot):
+        return send(x_hbm.at[place(m, 1 - x)], xb.at[at(m), lanes(x)], bulk_s.at[0], x_r.at[slot], peer)
 
     def y_local(p, m):
         return pltpu.make_async_copy(
             y_hbm.at[p, place(m, x)], panels[p].at[at(m), lanes(c)], y_r.at[p, index(m)])
 
-    def y_peer(p, m):
+    def y_peer(p, m, slot):
         return send(
-            y_hbm.at[p, place(m, 1 - x)], panels[p].at[at(m), lanes(c)], bulk_s.at[1], py_r.at[p, index(m)], peer)
+            y_hbm.at[p, place(m, 1 - x)], panels[p].at[at(m), lanes(c)], bulk_s.at[1], py_r.at[p, slot], peer)
 
     def y_mate(p, m):
         return send(
@@ -125,19 +125,31 @@
         pltpu.make_async_copy(block, block, y_r.at[p, index(m)]).wait()
 
     def pass_on(p, m):
-        y_peer(p, m).wait_recv()
+        y_peer(p, m, index(m)).wait_recv()
         y_forward(p, m).start()
 
+    def cut(m):
+        n = m[1] // CUTS
+        return [(m[0] + i * n, n) for i in range(CUTS)]
+
+    def send_x(m):
+        for part in cut(m):
+            x_peer(part, index(m)).start()
+
+    def send_y(p, m):
+        for part in cut(m):
+            y_peer(p, part, index(m)).start()
+
     def send_bulk(m):
-        x_peer(m).start()
-        y_peer(1, m).start()
-        y_peer(0, m).start()
+        send_x(m)
+        send_y(1, m)
+        send_y(0, m)
 
     for m in must:
-        x_peer(m).start()
-        y_peer(1, m).start()
+        send_x(m)
+        send_y(1, m)
     for m in must[:ahead]:
-        y_peer(0, m).start()
+        send_y(0, m)
     for m in must + extras:
         x_local(m).start()
         for p in (1, 0):
@@ -274,7 +286,7 @@
     a0.relay()
     a0.swap()
     for m in must[ahead:]:
-        y_peer(0, m).start()
+        send_y(0, m)
     for m in early:
         send_bulk(m)
     for m in must[:-2]:
@@ -423,7 +435,7 @@
         multiply_far(g, j)
         if j == len(sent) - 1:
             last.append(scatter(g))
-        elif g and j == len(sent) - 2:
+        elif g and j == len(sent) - 2 and g < len(parts) - 1:
             last[g - 1].relay()
 
     for t, (g, j) in enumerate(todo):
@@ -455,9 +467,10 @@
         done.drain()
 
 
+CUTS = 2
 CHUNK = 4
 AHEAD = 3
-EARLY = (3,)
+EARLY = (4,)
 LATE = (2,)
 PARTS = (2, 1, 1)
 UNITS = 16
@@ -484,8 +497,8 @@
     late = ranges(half + sum(n for _, n in early), LATE)
     extra = sum(EARLY) + sum(LATE)
     kept = ranges(0, (extra,))
-    first = (UNITS - extra) % CHUNK
-    sent = ranges(extra * unit, ((first,) if first else ()) + (CHUNK,) * ((UNITS - extra) // CHUNK))
+    rest = (UNITS - extra) % CHUNK
+    sent = ranges(extra * unit, (CHUNK,) * ((UNITS - extra) // CHUNK) + ((rest,) if rest else ()))
     held = half + extra * unit
     away = half - extra * unit
     wide = 2 * bw

time: 147 us -> 145 us (0.986)
  Pallas kernels: 144 us -> 142 us
    pallas_call x1, Pallas kernels: 144 us -> 142 us  [on_grid(): pl.pallas_call(functools.partial(whole_kernel, (nz, q, nq, AHEAD, early,...]
where the time goes in v5:
time: 145 us
  Pallas kernels  142 us (98%)
  local copies, waits for them, and re-layouts  1.98 us (1%)
    pallas_call x1, Pallas kernels, on_grid(): pl.pallas_call(functools.partial(whole_kernel, (nz, q, nq, AHEAD, early,...  142 us

profile of v5, /device:TPU:0, one launch (start us, length us, event | category | flops | bytes accessed | tf_op | source)
XLA Modules:
  0.0 145.0 jit_solution(14698050476296930873)
XLA Ops:
  0.6 142.4 %whole.1 = (f32[4096,128]{1,0:T(8,128)S(1)}, f32[64,512]{1,0:T(8,128)S(1)}) custom-call(f32[4096,128]{1,0:T(8,128)} %x_hbm.1, f32[2,4096,128]{2,1,0:T(8,128)} %y_hbm.1, f32[2,512,512]{2,1,0:T(8,128)} %t_hbm.1, f32[512,4096]{1,0:T(8,128)} %s_hbm.1), custom_call_target="tpu_custom_call" | custom-call | tf_op jit(solution)/shard_map/whole/pallas_call | solution.py:515
  143.0 1.3 copy.8
  144.3 0.7 copy.9

commit v6 on v5

--- a/solution.py
+++ b/solution.py
@@ -33,7 +33,15 @@
         return lax.dot_general(a, b, (dims, ((), ())), preferred_element_type=jnp.float32)
 
     (lh, ll), (rh, rl) = left, right
-    return one(lh, rh) + (one(lh, rl) + one(ll, rh))
+    free = 1 - dims[0][0]
+    size = lh.shape[free]
+    if size > STACK:
+        return one(lh, rh) + (one(lh, rl) + one(ll, rh))
+    stacked = one(jnp.concatenate([lh, ll], axis=free), rh)
+    return stacked[:size] + (one(lh, rl) + stacked[size:])
+
+
+STACK = 256
 
 
 def whole_kernel(
@@ -330,6 +338,8 @@
         take(m)
     a1.forward()
     a2.forward()
+    for m in early:
+        extra_inner(m)
 
     def band(g):
         return pl.ds(*spans[g])
@@ -384,7 +394,6 @@
     for m in late:
         take(m)
     for m in early:
-        extra_inner(m)
         wait_y(0, m)
         finish(everything, m)
         v_mate(0, everything, m).start()
@@ -448,10 +457,11 @@
     arrived(*todo[-1])
     for m in locals_[len(todo):]:
         write_out(m)
-    for one in last:
+    for one in last[:-1]:
         one.relay()
     for m in far:
         write_out(m)
+    last[-1].relay()
     for g in range(len(parts) - 1):
         collect(g)
     for s in (a0, a1, a2):

time: 145 us -> 144 us (level)
  no operation moved by 1% of the time
where the time goes in v6:
time: 144 us
  Pallas kernels  141 us (98%)
  local copies, waits for them, and re-layouts  1.98 us (1%)
    pallas_call x1, Pallas kernels, on_grid(): pl.pallas_call(functools.partial(whole_kernel, (nz, q, nq, AHEAD, early,...  141 us

profile of v6, /device:TPU:0, one launch (start us, length us, event | category | flops | bytes accessed | tf_op | source)
XLA Modules:
  0.0 143.8 jit_solution(6870978558971261491)
XLA Ops:
  0.6 141.2 %whole.1 = (f32[4096,128]{1,0:T(8,128)S(1)}, f32[64,512]{1,0:T(8,128)S(1)}) custom-call(f32[4096,128]{1,0:T(8,128)} %x_hbm.1, f32[2,4096,128]{2,1,0:T(8,128)} %y_hbm.1, f32[2,512,512]{2,1,0:T(8,128)} %t_hbm.1, f32[512,4096]{1,0:T(8,128)} %s_hbm.1), custom_call_target="tpu_custom_call" | custom-call | tf_op jit(solution)/shard_map/whole/pallas_call | solution.py:525
  141.8 1.3 copy.8
  143.2 0.7 copy.9

commit v7 on v6

--- a/solution.py
+++ b/solution.py
@@ -327,11 +327,11 @@
         inner(m)
     a2.relay()
     a1.swap()
-    for m in must[2:]:
-        inner(m)
     a2.swap()
     for m in late:
         send_bulk(m)
+    for m in must[2:]:
+        inner(m)
     a1.gather()
     a2.gather()
     for m in early:

time: 144 us -> 144 us (level)
  no operation moved by 1% of the time
where the time goes in v7:
time: 144 us
  Pallas kernels  141 us (98%)
  local copies, waits for them, and re-layouts  1.98 us (1%)
    pallas_call x1, Pallas kernels, on_grid(): pl.pallas_call(functools.partial(whole_kernel, (nz, q, nq, AHEAD, early,...  141 us

profile of v7, /device:TPU:0, one launch (start us, length us, event | category | flops | bytes accessed | tf_op | source)
XLA Modules:
  0.0 143.8 jit_solution(15242656654815664037)
XLA Ops:
  0.6 141.2 %whole.1 = (f32[4096,128]{1,0:T(8,128)S(1)}, f32[64,512]{1,0:T(8,128)S(1)}) custom-call(f32[4096,128]{1,0:T(8,128)} %x_hbm.1, f32[2,4096,128]{2,1,0:T(8,128)} %y_hbm.1, f32[2,512,512]{2,1,0:T(8,128)} %t_hbm.1, f32[512,4096]{1,0:T(8,128)} %s_hbm.1), custom_call_target="tpu_custom_call" | custom-call | tf_op jit(solution)/shard_map/whole/pallas_call | solution.py:525
  141.8 1.3 copy.8
  143.2 0.7 copy.9
